TPU v7x, 32 devices: a whole 2x2x4 slice. The times are simulated.
32 devices in a mesh: dp: 2 (over x), tp: 16 (over y, z, core).
Axes of the slice: x: 2, y: 2, z: 4, core: 2. Of those that a mesh axis runs over, the one named last changes fastest.
Arguments:
- x: bfloat16 [4096, 7168], P('dp'), parts along dimension 0
- w_gate: bfloat16 [7168, 20480], P(None, 'tp')
- w_up: bfloat16 [7168, 20480], P(None, 'tp')
- w_down: bfloat16 [20480, 7168], P('tp')
Outputs:
- output: bfloat16 [4096, 7168], P('dp'), parts along dimension 0
There are 2 independent parts. A program takes and returns all parts, laid end to end along the dimension named above; an argument that names none is the same for every part.
All inputs are finite; a program needn't handle non-finite values.
Results may differ from a plain program's by a relative error of at most 0.016.
Values are sent between devices in bfloat16 or wider.
A program may use at most 2 GiB of HBM per device.

v0:
```python
import jax
import jax.numpy as jnp
from jax import lax
from jax.sharding import PartitionSpec as P


def solution(mesh):
    def step(x, w_gate, w_up, w_down):
        gate = jnp.dot(x, w_gate, preferred_element_type=jnp.float32)
        up = jnp.dot(x, w_up, preferred_element_type=jnp.float32)
        hidden = (jax.nn.silu(gate) * up).astype(jnp.bfloat16)
        term = jnp.dot(hidden, w_down, preferred_element_type=jnp.float32).astype(jnp.bfloat16)
        return lax.psum(term, "tp")

    return jax.shard_map(
        step,
        mesh=mesh,
        in_specs=(P("dp", None), P(None, "tp"), P(None, "tp"), P("tp", None)),
        out_specs=P("dp", None),
        check_vma=False,
    )
```

profile of v0, /device:TPU:0, one launch (start us, length us, event | category | flops | bytes accessed | tf_op | source)
XLA Modules:
  0.0 678.2 jit_solution(16504848194098811774)
XLA Ops:
  6.5 0.0 all-reduce.2.cloned.1.call-start
  6.5 46.7 %fusion.1 = f32[2048,1280]{1,0:T(8,128)} fusion(bf16[2048,7168]{1,0:T(8,128)(2,1)} %param.4, bf16[7168,1280]{1,0:T(8,128)(2,1)} %param.5), kind=kOutput, calls=%fused_computation.3 | convolution fusion | flops 37580963840 | bytes 58195968 | tf_op jit(solution)/shard_map/dot_general | solution.py:9
  53.3 48.1 %fusion = bf16[2048,1280]{1,0:T(8,128)(2,1)S(1)} fusion(bf16[2048,7168]{1,0:T(8,128)(2,1)} %param.4, bf16[7168,1280]{1,0:T(8,128)(2,1)} %param.6, f32[2048,1280]{1,0:T(8,128)} %fusion.1), kind=kOutput, calls=%fused_computation.2 | convolution fusion | flops 37596692480 | bytes 63438848 | tf_op jit(solution)/shard_map/dot_general | solution.py:10
  101.3 46.9 %convolution_convert_fusion = bf16[2048,7168]{1,0:T(8,128)(2,1)} fusion(bf16[2048,1280]{1,0:T(8,128)(2,1)S(1)} %fusion, bf16[1280,7168]{1,0:T(8,128)(2,1)} %param.7), kind=kOutput, calls=%fused_computation | convolution fusion | flops 37595643904 | bytes 52953088 | tf_op jit(solution)/shard_map/dot_general | solution.py:12
  148.2 0.0 all-reduce.2.cloned.1.call-update
  148.3 502.9 %all-reduce.2.cloned.1.call-done = bf16[2048,7168]{1,0:T(8,128)(2,1)} async-done(((bf16[2048,7168]{1,0:T(8,128)(2,1)}), bf16[2048,7168]{1,0:T(8,128)(2,1)}) %all-reduce.2.cloned.1.call-update) | async-done | bytes 29360144 | tf_op jit(solution)/shard_map/psum | solution.py:13
  651.2 20.1 %copy.6 = bf16[2048,7168]{1,0:T(8,128)(2,1)} copy(bf16[2048,7168]{1,0:T(8,128)(2,1)} %all-reduce.2.cloned.1.call-done) | data formatting | bytes 58720256
Async XLA Ops:
  6.5 644.6 %all-reduce.2.cloned.1.call-start = ((), (), s32[]{:S(2)}) async-start(), calls=%async_computation | async-start | bytes 58720256 | tf_op jit(solution)/shard_map/psum | solution.py:13
Sparse Core Ops, SparseCore 0:
  148.4 502.7 all-reduce.1
where the time goes:
time: 678 us
  waiting for transfers between devices  503 us (74%)
  matrix products  142 us (21%)
  local copies, waits for them, and re-layouts  20.1 us (3%)
  between operations  13.4 us (2%)
    psum x1, waiting for transfers between devices, step(): return lax.psum(term, 'tp')  503 us
    dot_general x1, matrix products, step(): up = jnp.dot(x, w_up, preferred_element_type=jnp.float32)  48.1 us
    dot_general x1, matrix products, step(): jnp.dot(hidden, w_down, preferred_element_type=jnp.float32)  46.9 us
    dot_general x1, matrix products, step(): gate = jnp.dot(x, w_gate, preferred_element_type=jnp.float32)  46.7 us
    unnamed x1, local copies, waits for them, and re-layouts  20.1 us
  transfers between devices with their start and end apart: 1, of which 1 were waited for; matrix products, arithmetic and copies ran while one was open for 0% of the time, Pallas kernels for 0%

commit v1 on v0

v1 whole, which is shorter than its diff:
```python
import functools

import jax
import jax.numpy as jnp
from jax import lax
from jax.experimental import pallas as pl
from jax.experimental.pallas import tpu as pltpu
from jax.sharding import PartitionSpec as P

MESH = pl.DeviceIdType.MESH
F32, BF16 = jnp.float32, jnp.bfloat16
SLOTS = 4


def _tree(unit):
    parent = {}
    for y in range(2):
        for z in range(4):
            p = 4 * y + z
            if unit < 4:
                line = unit // 2
                root = 1 + line
                if y != line:
                    parent[p] = 4 * line + z
                else:
                    parent[p] = None if z == root else (p + 1 if z < root else p - 1)
            else:
                q = unit - 4
                if z != q:
                    parent[p] = p + 1 if z < q else p - 1
                else:
                    parent[p] = None if y == q % 2 else 4 * (1 - y) + z
    children = {p: [c for c in range(8) if parent[c] == p] for p in range(8)}

    def height(p):
        return 1 + max((height(c) for c in children[p]), default=-1)

    def depth(p):
        return 0 if parent[p] is None else 1 + depth(parent[p])

    return parent, children, [height(p) for p in range(8)], [depth(p) for p in range(8)]


TREES = [_tree(u) for u in range(8)]


def _landing(unit, p, k):
    if unit < 4:
        return 3 * (unit % 2) + k
    z, q = p % 4, unit - 4
    return k if z == q else 2 + (q - z) % 4


MAX_HEIGHT = max(max(t[2]) for t in TREES)
MAX_DEPTH = max(max(t[3]) for t in TREES)

ORDER = (
    ("X", 4), ("d", 0), ("d", 1), ("R", 0, 1), ("d", 2), ("R", 3, 2), ("d", 3), ("B", 3, 3), ("d", 4), ("R", 1, 1), ("d", 5),
    ("R", 4, 2), ("B", 1, 2), ("d", 6), ("S", 0), ("g", 0), ("B", 4, 3), ("F", 3), ("g", 1), ("R", 2, 1), ("B", 2, 2), ("g", 2),
)


def _kernel(cfg, x_hbm, wg_hbm, wu_hbm, wd_hbm, y_hbm, xb, wgb, wub, wdb, hb, own, stage, pbuf, sbuf, fbuf, ry, rz,
            xsem, gsem, usem, dsem, stsem, psem, ssem, rysem, rzsem, bsem, ysem, fssem, frsem):
    nb, rows, half_cols, yc, zc, gw, dt = (cfg[k] for k in ("nb", "rows", "half", "yc", "zc", "gw", "dt"))
    mine = rows // 2
    ng = wg_hbm.shape[1] // gw
    nt = half_cols // dt
    wslots = wdb.shape[0]
    chunks = 2 * nb

    dp = lax.axis_index("dp")
    me = lax.axis_index("tp")
    core = me % 2
    pos = me // 2
    partner = me + 1 - 2 * core

    def select(values):
        values = [0 if v is None else v for v in values]
        if all(v == values[0] for v in values):
            return values[0]
        out = jnp.int32(values[0])
        for p in range(1, 8):
            out = jnp.where(pos == p, jnp.int32(values[p]), out)
        return out

    def among(positions):
        out = pos == positions[0]
        for p in positions[1:]:
            out = jnp.logical_or(out, pos == p)
        return out

    def remote(src, dst, send, recv, device):
        return pltpu.make_async_remote_copy(
            src_ref=src, dst_ref=dst, send_sem=send, recv_sem=recv, device_id=(dp, device), device_id_type=MESH
        )

    def columns(u):
        return slice(u * yc, (u + 1) * yc) if u < 4 else slice(4 * yc + (u - 4) * zc, 4 * yc + (u - 3) * zc)

    def landed(u, slot, index):
        return (ry.at[slot, index], rysem.at[slot, index]) if u < 4 else (rz.at[slot, index], rzsem.at[slot, index])

    def load_x(b):
        slot = b % 2
        first = pl.multiple_of(b * rows + core * mine, mine)
        second = pl.multiple_of(b * rows + (1 - core) * mine, mine)
        return (
            pltpu.make_async_copy(x_hbm.at[pl.ds(first, mine)], xb.at[slot, pl.ds(0, mine)], xsem.at[slot, 0]),
            pltpu.make_async_copy(x_hbm.at[pl.ds(second, mine)], xb.at[slot, pl.ds(mine, mine)], xsem.at[slot, 1]),
        )

    def load_g(s):
        slot = s % 2
        cols = pl.ds(pl.multiple_of((s % ng) * gw, gw), gw)
        return (
            pltpu.make_async_copy(wg_hbm.at[:, cols], wgb.at[slot], gsem.at[slot]),
            pltpu.make_async_copy(wu_hbm.at[:, cols], wub.at[slot], usem.at[slot]),
        )

    def load_d(t):
        slot = t % wslots
        cols = pl.ds(pl.multiple_of((t % (2 * nt)) * dt, dt), dt)
        return (pltpu.make_async_copy(wd_hbm.at[:, cols], wdb.at[slot], dsem.at[slot]),)

    def start(copies):
        for copy in copies:
            copy.start()

    def wait(copies):
        for copy in copies:
            copy.wait()

    def gate_step(b, g):
        s = b * ng + g
        slot = s % 2
        wait(load_g(s))
        xv = xb.at[b % 2]
        gate = jnp.dot(xv[...], wgb[slot], preferred_element_type=F32)
        up = jnp.dot(xv[...], wub[slot], preferred_element_type=F32)
        hb[b % 2, :, pl.ds(pl.multiple_of(g * gw, gw), gw)] = (jax.nn.silu(gate) * up).astype(BF16)

        @pl.when(s + 2 < nb * ng)
        def _():
            start(load_g(s + 2))

    def down_step(b, half, j):
        t = b * 2 * nt + half * nt + j
        slot = (2 * b + half) % SLOTS
        wait(load_d(t))
        term = jnp.dot(hb[b % 2], wdb[t % wslots], preferred_element_type=F32)
        cols = slice(j * dt, (j + 1) * dt)
        own[slot, :, cols] = term[:mine]
        stage[slot, :, cols] = term[mine:].astype(BF16)

        @pl.when(t + wslots < nb * 2 * nt)
        def _():
            start(load_d(t + wslots))

    def to_partner(slot):
        return remote(stage.at[slot], pbuf.at[slot], stsem.at[slot], psem.at[slot], partner)

    def up_copy(u, slot):
        parent = TREES[u][0]
        place = [None if parent[p] is None else _landing(u, parent[p], TREES[u][1][parent[p]].index(p)) for p in range(8)]
        dst, sem = landed(u, slot, select(place))
        target = 2 * select([parent[p] for p in range(8)]) + core
        return remote(sbuf.at[slot, :, columns(u)], dst, ssem.at[slot, u, 0], sem, target)

    def down_copy(u, slot, k):
        children = TREES[u][1]
        target = 2 * select([children[p][k] if k < len(children[p]) else None for p in range(8)]) + core
        piece = fbuf.at[slot, :, columns(u)]
        return remote(piece, piece, ssem.at[slot, u, 1 + k], bsem.at[slot, u], target)

    def groups(u, level, kind):
        parent, children, height, depth = TREES[u]
        found = {}
        for p in range(8):
            if (height if kind == "R" else depth)[p] == level:
                found.setdefault((parent[p] is None, len(children[p])), []).append(p)
        return sorted(found.items())

    def reduce_level(slot, level):
        if level == 0:
            to_partner(slot).wait_recv()
        for u in range(8):
            for (root, count), positions in groups(u, level, "R"):

                @pl.when(among(positions))
                def _(u=u, root=root, count=count):
                    cols = columns(u)
                    total = own[slot, :, cols] + pbuf[slot, :, cols].astype(F32)
                    for k in range(count):
                        index = select([_landing(u, p, k) for p in range(8)])
                        src, sem = landed(u, slot, index)
                        remote(src, src, ssem.at[slot, u, 0], sem, me).wait_recv()
                        total = total + src[...].astype(F32)
                    out = fbuf if root else sbuf
                    out[slot, :, cols] = total.astype(BF16)
                    if root:
                        for k in range(count):
                            down_copy(u, slot, k).start()
                    else:
                        up_copy(u, slot).start()

    def broadcast_level(slot, level):
        for u in range(8):
            for (_, count), positions in groups(u, level, "B"):

                @pl.when(among(positions))
                def _(u=u, count=count):
                    down_copy(u, slot, 0).wait_recv()
                    for k in range(count):
                        down_copy(u, slot, k).start()

    def finished(c, parity):
        slot = c % SLOTS
        piece = y_hbm.at[
            pl.ds(pl.multiple_of((c // 2) * rows + core * mine, mine), mine), pl.ds(parity * half_cols, half_cols)
        ]
        return (
            pltpu.make_async_copy(fbuf.at[slot], piece, ysem.at[slot]),
            remote(fbuf.at[slot], piece, fssem.at[slot], frsem.at[slot], partner),
        )

    def settle(c, parity):
        slot = c % SLOTS
        to_partner(slot).wait_send()
        for u in range(8):
            parent, children, _, _ = TREES[u]

            @pl.when(among([p for p in range(8) if parent[p] is not None]))
            def _(u=u):
                up_copy(u, slot).wait_send()

            for k in range(3):
                have = [p for p in range(8) if len(children[p]) > k]
                if have:

                    @pl.when(among(have))
                    def _(u=u, k=k):
                        down_copy(u, slot, k).wait_send()

        local, other = finished(c, parity)
        local.wait()
        other.wait()

    start(load_x(0))
    start(load_g(0))
    start(load_g(1))
    start(load_x(1))
    for t in range(wslots):
        start(load_d(t))

    barrier = pltpu.get_barrier_semaphore()
    z = pos % 4
    rung = (me + 8) % 16

    def greet(device):
        pl.semaphore_signal(barrier, inc=1, device_id=(dp, device), device_id_type=MESH)

    greet(partner)
    greet(rung)

    @pl.when(z > 0)
    def _():
        greet(me - 2)

    @pl.when(z < 3)
    def _():
        greet(me + 2)

    pl.semaphore_wait(barrier, 3 + jnp.where(jnp.logical_or(z == 0, z == 3), 0, 1))

    wait(load_x(0))

    @pl.loop(0, ng)
    def _(g):
        gate_step(0, g)

    split = (ng + 1) // 2

    @pl.loop(0, nb + 2)
    def _(b):
        computing = b < nb
        more = b + 1 < nb

        @pl.when(b + 2 < nb)
        def _():
            start(load_x(b + 2))

        @pl.when(more)
        def _():
            wait(load_x(b + 1))

        for half in range(2):
            for item in cfg["order"]:
                kind = item[0]
                if kind == "d":
                    if item[1] < nt:

                        @pl.when(computing)
                        def _(half=half, j=item[1]):
                            down_step(b, half, j)

                elif kind == "g":
                    g = item[1] + (split if half else 0)
                    if g < (ng if half else split):

                        @pl.when(more)
                        def _(g=g):
                            gate_step(b + 1, g)

                else:
                    lag = item[-1]
                    c = 2 * b + half - lag
                    parity = (half - lag) % 2

                    @pl.when(jnp.logical_and(c >= 0, c < chunks))
                    def _(kind=kind, item=item, c=c, parity=parity):
                        slot = c % SLOTS
                        if kind == "S":
                            to_partner(slot).start()
                        elif kind == "R":
                            reduce_level(slot, item[1])
                        elif kind == "B":
                            broadcast_level(slot, item[1])
                        elif kind == "F":
                            start(finished(c, parity))
                        elif kind == "X":
                            settle(c, parity)


def build(mesh, cfg):
    def step(x, w_gate, w_up, w_down):
        d = x.shape[1]
        rows, mine = cfg["rows"], cfg["rows"] // 2
        hidden = w_gate.shape[1]
        dma = pltpu.SemaphoreType.DMA
        any_spec = pl.BlockSpec(memory_space=pl.ANY)
        return pl.pallas_call(
            functools.partial(_kernel, cfg),
            name="mlp",
            out_shape=jax.ShapeDtypeStruct(x.shape, BF16),
            in_specs=[any_spec] * 4,
            out_specs=any_spec,
            scratch_shapes=[
                pltpu.VMEM((2, rows, d), BF16),
                pltpu.VMEM((2, d, cfg["gw"]), BF16),
                pltpu.VMEM((2, d, cfg["gw"]), BF16),
                pltpu.VMEM((4, hidden, cfg["dt"]), BF16),
                pltpu.VMEM((2, rows, hidden), BF16),
                pltpu.VMEM((SLOTS, mine, cfg["half"]), F32),
                pltpu.VMEM((SLOTS, mine, cfg["half"]), BF16),
                pltpu.VMEM((SLOTS, mine, cfg["half"]), BF16),
                pltpu.VMEM((SLOTS, mine, cfg["half"]), BF16),
                pltpu.VMEM((SLOTS, mine, cfg["half"]), BF16),
                pltpu.VMEM((SLOTS, 6, mine, cfg["yc"]), BF16),
                pltpu.VMEM((SLOTS, 6, mine, cfg["zc"]), BF16),
                dma((2, 2)),
                dma((2,)),
                dma((2,)),
                dma((4,)),
                dma((SLOTS,)),
                dma((SLOTS,)),
                dma((SLOTS, 8, 4)),
                dma((SLOTS, 6)),
                dma((SLOTS, 6)),
                dma((SLOTS, 8)),
                dma((SLOTS,)),
                dma((SLOTS,)),
                dma((SLOTS,)),
            ],
            compiler_params=pltpu.CompilerParams(
                collective_id=0, has_side_effects=True, vmem_limit_bytes=67043328
            ),
        )(x, w_gate, w_up, w_down)

    return jax.shard_map(
        step,
        mesh=mesh,
        in_specs=(P("dp", None), P(None, "tp"), P(None, "tp"), P("tp", None)),
        out_specs=P("dp", None),
        check_vma=False,
    )


def solution(mesh):
    return build(mesh, dict(nb=8, rows=256, half=3584, yc=512, zc=384, gw=256, dt=512, order=ORDER))
```

time: 678 us -> 427 us (0.63)
  waiting for transfers between devices: 503 us -> 0 us
  Pallas kernels: 0 us -> 406 us
  matrix products: 142 us -> 0 us
  between operations: 13.4 us -> 0.01 us
    psum x1 -> x0, waiting for transfers between devices: 503 us -> none  [step(): return lax.psum(term, 'tp')]
    pallas_call x0 -> x1, Pallas kernels: none -> 406 us  [step(): pl.pallas_call(functools.partial(_kernel, cfg), name='mlp', out_shape=jax...]
    dot_general x3 -> x0, matrix products: 142 us -> none  [the longest x1 48.1 us: step(): up = jnp.dot(x, w_up, preferred_element_type=jnp.float32)]
  transfers between devices with their start and end apart: 1 -> 0, of which waited for: 1 -> 0; matrix products, arithmetic and copies ran while one was open for 0% -> 0% of each run, Pallas kernels for 0% -> 0%
where the time goes in v1:
time: 427 us
  Pallas kernels  406 us (95%)
  local copies, waits for them, and re-layouts  20.2 us (5%)
    pallas_call x1, Pallas kernels, step(): pl.pallas_call(functools.partial(_kernel, cfg), name='mlp', out_shape=jax...  406 us
    unnamed x1, local copies, waits for them, and re-layouts  20.2 us

profile of v1, /device:TPU:0, one launch (start us, length us, event | category | flops | bytes accessed | tf_op | source)
XLA Modules:
  0.0 426.6 jit_solution(3298978333213099036)
XLA Ops:
  0.0 406.4 %mlp.1 = bf16[2048,7168]{1,0:T(8,128)(2,1)} custom-call(bf16[2048,7168]{1,0:T(8,128)(2,1)} %x_hbm.1, bf16[7168,1280]{1,0:T(8,128)(2,1)} %wg_hbm.1, bf16[7168,1280]{1,0:T(8,128)(2,1)} %wu_hbm.1, bf16[1280,7168]{1,0:T(8,128)(2,1)} %wd_hbm.1), custom_call_target="tpu_custom_call" | custom-call | tf_op jit(solution)/shard_map/mlp/pallas_call | solution.py:342
  406.4 20.2 %copy.6 = bf16[2048,7168]{1,0:T(8,128)(2,1)} copy(bf16[2048,7168]{1,0:T(8,128)(2,1)} %mlp.1) | data formatting | bytes 58720256

commit v2 on v1

--- a/solution.py
+++ b/solution.py
@@ -9,7 +9,6 @@
 
 MESH = pl.DeviceIdType.MESH
 F32, BF16 = jnp.float32, jnp.bfloat16
-SLOTS = 4
 
 
 def _tree(unit):
@@ -51,17 +50,21 @@
     return k if z == q else 2 + (q - z) % 4
 
 
-MAX_HEIGHT = max(max(t[2]) for t in TREES)
-MAX_DEPTH = max(max(t[3]) for t in TREES)
-
 ORDER = (
-    ("X", 4), ("d", 0), ("d", 1), ("R", 0, 1), ("d", 2), ("R", 3, 2), ("d", 3), ("B", 3, 3), ("d", 4), ("R", 1, 1), ("d", 5),
-    ("R", 4, 2), ("B", 1, 2), ("d", 6), ("S", 0), ("g", 0), ("B", 4, 3), ("F", 3), ("g", 1), ("R", 2, 1), ("B", 2, 2), ("g", 2),
+    ("R", 0, (0, 2), 1), ("R", 3, (0, 2), 2), ("d", 0), ("R", 3, (5, 6), 2), ("F", 5), ("d", 1), ("d", 2), ("R", 0, (4, 7), 1),
+    ("R", 0, (1, 3), 1), ("R", 1, (4, 7), 1), ("B", 2, (5, 6), 3), ("B", 3, (4, 7), 4), ("R", 3, (1, 3), 2),
+    ("R", 0, (5, 6), 1), ("d", 3), ("B", 3, (0, 2), 4), ("B", 2, (4, 7), 3), ("g", 0), ("B", 3, (1, 3), 4),
+    ("R", 3, (4, 7), 2), ("d", 4), ("R", 1, (0, 2), 1), ("B", 2, (0, 2), 3), ("d", 5), ("R", 1, (5, 6), 1),
+    ("B", 2, (1, 3), 3), ("R", 4, (4, 7), 2), ("d", 6), ("B", 1, (0, 2), 2), ("S", 0), ("B", 1, (5, 6), 2), ("g", 1),
+    ("R", 2, (0, 2), 1), ("R", 2, (4, 7), 1), ("R", 2, (5, 6), 1), ("R", 1, (1, 3), 1), ("B", 4, (4, 7), 4), ("g", 2),
+    ("R", 2, (1, 3), 1), ("B", 1, (1, 3), 2), ("B", 3, (5, 6), 4), ("B", 1, (4, 7), 2),
 )
+OWN, STAGE, PBUF, SBUF, FBUF, RBUF = 3, 2, 4, 4, 6, 4
+HAND = min((item[3], k) for k, item in enumerate(ORDER) if item[0] == "R")[1]
 
 
 def _kernel(cfg, x_hbm, wg_hbm, wu_hbm, wd_hbm, y_hbm, xb, wgb, wub, wdb, hb, own, stage, pbuf, sbuf, fbuf, ry, rz,
-            xsem, gsem, usem, dsem, stsem, psem, ssem, rysem, rzsem, bsem, ysem, fssem, frsem):
+            xsem, gsem, usem, dsem, stsem, psem, upsem, downsem, rysem, rzsem, bsem, ysem, fssem, frsem):
     nb, rows, half_cols, yc, zc, gw, dt = (cfg[k] for k in ("nb", "rows", "half", "yc", "zc", "gw", "dt"))
     mine = rows // 2
     ng = wg_hbm.shape[1] // gw
@@ -98,7 +101,8 @@
     def columns(u):
         return slice(u * yc, (u + 1) * yc) if u < 4 else slice(4 * yc + (u - 4) * zc, 4 * yc + (u - 3) * zc)
 
-    def landed(u, slot, index):
+    def landed(u, c, index):
+        slot = c % RBUF
         return (ry.at[slot, index], rysem.at[slot, index]) if u < 4 else (rz.at[slot, index], rzsem.at[slot, index])
 
     def load_x(b):
@@ -146,32 +150,32 @@
 
     def down_step(b, half, j):
         t = b * 2 * nt + half * nt + j
-        slot = (2 * b + half) % SLOTS
+        c = 2 * b + half
         wait(load_d(t))
         term = jnp.dot(hb[b % 2], wdb[t % wslots], preferred_element_type=F32)
         cols = slice(j * dt, (j + 1) * dt)
-        own[slot, :, cols] = term[:mine]
-        stage[slot, :, cols] = term[mine:].astype(BF16)
+        own[c % OWN, :, cols] = term[:mine]
+        stage[c % STAGE, :, cols] = term[mine:].astype(BF16)
 
         @pl.when(t + wslots < nb * 2 * nt)
         def _():
             start(load_d(t + wslots))
 
-    def to_partner(slot):
-        return remote(stage.at[slot], pbuf.at[slot], stsem.at[slot], psem.at[slot], partner)
-
-    def up_copy(u, slot):
+    def to_partner(c):
+        return remote(stage.at[c % STAGE], pbuf.at[c % PBUF], stsem.at[c % STAGE], psem.at[c % PBUF], partner)
+
+    def up_copy(u, c):
         parent = TREES[u][0]
         place = [None if parent[p] is None else _landing(u, parent[p], TREES[u][1][parent[p]].index(p)) for p in range(8)]
-        dst, sem = landed(u, slot, select(place))
+        dst, sem = landed(u, c, select(place))
         target = 2 * select([parent[p] for p in range(8)]) + core
-        return remote(sbuf.at[slot, :, columns(u)], dst, ssem.at[slot, u, 0], sem, target)
-
-    def down_copy(u, slot, k):
+        return remote(sbuf.at[c % SBUF, :, columns(u)], dst, upsem.at[c % SBUF, u], sem, target)
+
+    def down_copy(u, c, k):
         children = TREES[u][1]
         target = 2 * select([children[p][k] if k < len(children[p]) else None for p in range(8)]) + core
-        piece = fbuf.at[slot, :, columns(u)]
-        return remote(piece, piece, ssem.at[slot, u, 1 + k], bsem.at[slot, u], target)
+        piece = fbuf.at[c % FBUF, :, columns(u)]
+        return remote(piece, piece, downsem.at[c % FBUF, u, k], bsem.at[c % FBUF, u], target)
 
     def groups(u, level, kind):
         parent, children, height, depth = TREES[u]
@@ -181,41 +185,38 @@
                 found.setdefault((parent[p] is None, len(children[p])), []).append(p)
         return sorted(found.items())
 
-    def reduce_level(slot, level):
-        if level == 0:
-            to_partner(slot).wait_recv()
-        for u in range(8):
+    def reduce_level(c, level, units):
+        for u in units:
             for (root, count), positions in groups(u, level, "R"):
 
                 @pl.when(among(positions))
                 def _(u=u, root=root, count=count):
                     cols = columns(u)
-                    total = own[slot, :, cols] + pbuf[slot, :, cols].astype(F32)
+                    total = own[c % OWN, :, cols] + pbuf[c % PBUF, :, cols].astype(F32)
                     for k in range(count):
-                        index = select([_landing(u, p, k) for p in range(8)])
-                        src, sem = landed(u, slot, index)
-                        remote(src, src, ssem.at[slot, u, 0], sem, me).wait_recv()
+                        src, sem = landed(u, c, select([_landing(u, p, k) for p in range(8)]))
+                        remote(src, src, upsem.at[c % SBUF, u], sem, me).wait_recv()
                         total = total + src[...].astype(F32)
-                    out = fbuf if root else sbuf
-                    out[slot, :, cols] = total.astype(BF16)
                     if root:
+                        fbuf[c % FBUF, :, cols] = total.astype(BF16)
                         for k in range(count):
-                            down_copy(u, slot, k).start()
+                            down_copy(u, c, k).start()
                     else:
-                        up_copy(u, slot).start()
-
-    def broadcast_level(slot, level):
-        for u in range(8):
+                        sbuf[c % SBUF, :, cols] = total.astype(BF16)
+                        up_copy(u, c).start()
+
+    def broadcast_level(c, level, units):
+        for u in units:
             for (_, count), positions in groups(u, level, "B"):
 
                 @pl.when(among(positions))
                 def _(u=u, count=count):
-                    down_copy(u, slot, 0).wait_recv()
+                    down_copy(u, c, 0).wait_recv()
                     for k in range(count):
-                        down_copy(u, slot, k).start()
+                        down_copy(u, c, k).start()
 
     def finished(c, parity):
-        slot = c % SLOTS
+        slot = c % FBUF
         piece = y_hbm.at[
             pl.ds(pl.multiple_of((c // 2) * rows + core * mine, mine), mine), pl.ds(parity * half_cols, half_cols)
         ]
@@ -224,23 +225,23 @@
             remote(fbuf.at[slot], piece, fssem.at[slot], frsem.at[slot], partner),
         )
 
-    def settle(c, parity):
-        slot = c % SLOTS
-        to_partner(slot).wait_send()
+    def settle_up(c):
         for u in range(8):
-            parent, children, _, _ = TREES[u]
+            parent = TREES[u][0]
 
             @pl.when(among([p for p in range(8) if parent[p] is not None]))
             def _(u=u):
-                up_copy(u, slot).wait_send()
-
+                up_copy(u, c).wait_send()
+
+    def settle_down(c, parity):
+        for u in range(8):
             for k in range(3):
-                have = [p for p in range(8) if len(children[p]) > k]
+                have = [p for p in range(8) if len(TREES[u][1][p]) > k]
                 if have:
 
                     @pl.when(among(have))
                     def _(u=u, k=k):
-                        down_copy(u, slot, k).wait_send()
+                        down_copy(u, c, k).wait_send()
 
         local, other = finished(c, parity)
         local.wait()
@@ -281,7 +282,7 @@
 
     split = (ng + 1) // 2
 
-    @pl.loop(0, nb + 2)
+    @pl.loop(0, nb + FBUF // 2)
     def _(b):
         computing = b < nb
         more = b + 1 < nb
@@ -295,8 +296,21 @@
             wait(load_x(b + 1))
 
         for half in range(2):
-            for item in cfg["order"]:
+
+            def after(lag, act, *args, half=half):
+                c = 2 * b + half - lag
+
+                @pl.when(jnp.logical_and(c >= 0, c < chunks))
+                def _():
+                    act(c, *args)
+
+            after(STAGE, lambda c: to_partner(c).wait_send())
+            after(SBUF, settle_up)
+            after(FBUF, settle_down, (half - FBUF) % 2)
+            for k, item in enumerate(cfg["order"]):
                 kind = item[0]
+                if k == HAND:
+                    after(item[3], lambda c: to_partner(c).wait_recv())
                 if kind == "d":
                     if item[1] < nt:
 
@@ -312,24 +326,14 @@
                         def _(g=g):
                             gate_step(b + 1, g)
 
-                else:
-                    lag = item[-1]
-                    c = 2 * b + half - lag
-                    parity = (half - lag) % 2
-
-                    @pl.when(jnp.logical_and(c >= 0, c < chunks))
-                    def _(kind=kind, item=item, c=c, parity=parity):
-                        slot = c % SLOTS
-                        if kind == "S":
-                            to_partner(slot).start()
-                        elif kind == "R":
-                            reduce_level(slot, item[1])
-                        elif kind == "B":
-                            broadcast_level(slot, item[1])
-                        elif kind == "F":
-                            start(finished(c, parity))
-                        elif kind == "X":
-                            settle(c, parity)
+                elif kind == "S":
+                    after(0, lambda c: to_partner(c).start())
+                elif kind == "R":
+                    after(item[3], reduce_level, item[1], item[2])
+                elif kind == "B":
+                    after(item[3], broadcast_level, item[1], item[2])
+                elif kind == "F":
+                    after(item[1], lambda c, parity: [p.start() for p in finished(c, parity)], (half - item[1]) % 2)
 
 
 def build(mesh, cfg):
@@ -351,26 +355,27 @@
                 pltpu.VMEM((2, d, cfg["gw"]), BF16),
                 pltpu.VMEM((4, hidden, cfg["dt"]), BF16),
                 pltpu.VMEM((2, rows, hidden), BF16),
-                pltpu.VMEM((SLOTS, mine, cfg["half"]), F32),
-                pltpu.VMEM((SLOTS, mine, cfg["half"]), BF16),
-                pltpu.VMEM((SLOTS, mine, cfg["half"]), BF16),
-                pltpu.VMEM((SLOTS, mine, cfg["half"]), BF16),
-                pltpu.VMEM((SLOTS, mine, cfg["half"]), BF16),
-                pltpu.VMEM((SLOTS, 6, mine, cfg["yc"]), BF16),
-                pltpu.VMEM((SLOTS, 6, mine, cfg["zc"]), BF16),
+                pltpu.VMEM((OWN, mine, cfg["half"]), F32),
+                pltpu.VMEM((STAGE, mine, cfg["half"]), BF16),
+                pltpu.VMEM((PBUF, mine, cfg["half"]), BF16),
+                pltpu.VMEM((SBUF, mine, cfg["half"]), BF16),
+                pltpu.VMEM((FBUF, mine, cfg["half"]), BF16),
+                pltpu.VMEM((RBUF, 6, mine, cfg["yc"]), BF16),
+                pltpu.VMEM((RBUF, 6, mine, cfg["zc"]), BF16),
                 dma((2, 2)),
                 dma((2,)),
                 dma((2,)),
                 dma((4,)),
-                dma((SLOTS,)),
-                dma((SLOTS,)),
-                dma((SLOTS, 8, 4)),
-                dma((SLOTS, 6)),
-                dma((SLOTS, 6)),
-                dma((SLOTS, 8)),
-                dma((SLOTS,)),
-                dma((SLOTS,)),
-                dma((SLOTS,)),
+                dma((STAGE,)),
+                dma((PBUF,)),
+                dma((SBUF, 8)),
+                dma((FBUF, 8, 3)),
+                dma((RBUF, 6)),
+                dma((RBUF, 6)),
+                dma((FBUF, 8)),
+                dma((FBUF,)),
+                dma((FBUF,)),
+                dma((FBUF,)),
             ],
             compiler_params=pltpu.CompilerParams(
                 collective_id=0, has_side_effects=True, vmem_limit_bytes=67043328

time: 427 us -> 313 us (0.73)
  Pallas kernels: 406 us -> 293 us
    pallas_call x1, Pallas kernels: 406 us -> 293 us  [step(): pl.pallas_call(functools.partial(_kernel, cfg), name='mlp', out_shape=jax...]
where the time goes in v2:
time: 313 us
  Pallas kernels  293 us (94%)
  local copies, waits for them, and re-layouts  20.2 us (6%)
    pallas_call x1, Pallas kernels, step(): pl.pallas_call(functools.partial(_kernel, cfg), name='mlp', out_shape=jax...  293 us
    unnamed x1, local copies, waits for them, and re-layouts  20.2 us

profile of v2, /device:TPU:0, one launch (start us, length us, event | category | flops | bytes accessed | tf_op | source)
XLA Modules:
  0.0 312.9 jit_solution(9424657459343928064)
XLA Ops:
  0.0 292.8 %mlp.1 = bf16[2048,7168]{1,0:T(8,128)(2,1)} custom-call(bf16[2048,7168]{1,0:T(8,128)(2,1)} %x_hbm.1, bf16[7168,1280]{1,0:T(8,128)(2,1)} %wg_hbm.1, bf16[7168,1280]{1,0:T(8,128)(2,1)} %wu_hbm.1, bf16[1280,7168]{1,0:T(8,128)(2,1)} %wd_hbm.1), custom_call_target="tpu_custom_call" | custom-call | tf_op jit(solution)/shard_map/mlp/pallas_call | solution.py:346
  292.8 20.2 %copy.6 = bf16[2048,7168]{1,0:T(8,128)(2,1)} copy(bf16[2048,7168]{1,0:T(8,128)(2,1)} %mlp.1) | data formatting | bytes 58720256

commit v3 on v2

--- a/solution.py
+++ b/solution.py
@@ -51,13 +51,13 @@
 
 
 ORDER = (
-    ("R", 0, (0, 2), 1), ("R", 3, (0, 2), 2), ("d", 0), ("R", 3, (5, 6), 2), ("F", 5), ("d", 1), ("d", 2), ("R", 0, (4, 7), 1),
-    ("R", 0, (1, 3), 1), ("R", 1, (4, 7), 1), ("B", 2, (5, 6), 3), ("B", 3, (4, 7), 4), ("R", 3, (1, 3), 2),
-    ("R", 0, (5, 6), 1), ("d", 3), ("B", 3, (0, 2), 4), ("B", 2, (4, 7), 3), ("g", 0), ("B", 3, (1, 3), 4),
-    ("R", 3, (4, 7), 2), ("d", 4), ("R", 1, (0, 2), 1), ("B", 2, (0, 2), 3), ("d", 5), ("R", 1, (5, 6), 1),
-    ("B", 2, (1, 3), 3), ("R", 4, (4, 7), 2), ("d", 6), ("B", 1, (0, 2), 2), ("S", 0), ("B", 1, (5, 6), 2), ("g", 1),
-    ("R", 2, (0, 2), 1), ("R", 2, (4, 7), 1), ("R", 2, (5, 6), 1), ("R", 1, (1, 3), 1), ("B", 4, (4, 7), 4), ("g", 2),
-    ("R", 2, (1, 3), 1), ("B", 1, (1, 3), 2), ("B", 3, (5, 6), 4), ("B", 1, (4, 7), 2),
+    ("d", 0), ("F", 5), ("R", 0, (1, 3), 1), ("B", 3, (0, 2), 4), ("B", 1, (1, 3), 3), ("d", 1), ("R", 3, (5, 6), 2),
+    ("d", 2), ("d", 3), ("R", 3, (4, 7), 2), ("B", 2, (1, 3), 4), ("R", 1, (4, 7), 1), ("R", 3, (0, 2), 2), ("g", 0),
+    ("B", 3, (4, 7), 4), ("R", 1, (0, 2), 1), ("d", 4), ("R", 1, (5, 6), 1), ("d", 5), ("B", 2, (4, 7), 3), ("d", 6),
+    ("R", 4, (4, 7), 2), ("R", 3, (1, 3), 2), ("S", 0), ("R", 1, (1, 3), 1), ("R", 2, (4, 7), 1), ("g", 1),
+    ("R", 2, (5, 6), 1), ("B", 1, (0, 2), 2), ("B", 2, (0, 2), 3), ("R", 2, (0, 2), 1), ("g", 2), ("B", 1, (5, 6), 2),
+    ("B", 2, (5, 6), 3), ("R", 0, (0, 2), 0), ("R", 0, (4, 7), 0), ("B", 4, (4, 7), 4), ("B", 1, (4, 7), 2),
+    ("R", 2, (1, 3), 1), ("B", 3, (5, 6), 4), ("B", 3, (1, 3), 4), ("R", 0, (5, 6), 0),
 )
 OWN, STAGE, PBUF, SBUF, FBUF, RBUF = 3, 2, 4, 4, 6, 4
 HAND = min((item[3], k) for k, item in enumerate(ORDER) if item[0] == "R")[1]
@@ -69,13 +69,13 @@
     mine = rows // 2
     ng = wg_hbm.shape[1] // gw
     nt = half_cols // dt
-    wslots = wdb.shape[0]
+    gslots, wslots = wgb.shape[0], wdb.shape[0]
     chunks = 2 * nb
 
     dp = lax.axis_index("dp")
     me = lax.axis_index("tp")
     core = me % 2
-    pos = me // 2
+    pos = me // 2 + core * (7 - 2 * (me // 2))
     partner = me + 1 - 2 * core
 
     def select(values):
@@ -93,9 +93,12 @@
             out = jnp.logical_or(out, pos == p)
         return out
 
-    def remote(src, dst, send, recv, device):
+    def device(position):
+        return 2 * (position + core * (7 - 2 * position)) + core
+
+    def remote(src, dst, send, recv, target):
         return pltpu.make_async_remote_copy(
-            src_ref=src, dst_ref=dst, send_sem=send, recv_sem=recv, device_id=(dp, device), device_id_type=MESH
+            src_ref=src, dst_ref=dst, send_sem=send, recv_sem=recv, device_id=(dp, target), device_id_type=MESH
         )
 
     def columns(u):
@@ -115,7 +118,7 @@
         )
 
     def load_g(s):
-        slot = s % 2
+        slot = s % gslots
         cols = pl.ds(pl.multiple_of((s % ng) * gw, gw), gw)
         return (
             pltpu.make_async_copy(wg_hbm.at[:, cols], wgb.at[slot], gsem.at[slot]),
@@ -137,16 +140,16 @@
 
     def gate_step(b, g):
         s = b * ng + g
-        slot = s % 2
+        slot = s % gslots
         wait(load_g(s))
         xv = xb.at[b % 2]
         gate = jnp.dot(xv[...], wgb[slot], preferred_element_type=F32)
         up = jnp.dot(xv[...], wub[slot], preferred_element_type=F32)
         hb[b % 2, :, pl.ds(pl.multiple_of(g * gw, gw), gw)] = (jax.nn.silu(gate) * up).astype(BF16)
 
-        @pl.when(s + 2 < nb * ng)
+        @pl.when(s + gslots < nb * ng)
         def _():
-            start(load_g(s + 2))
+            start(load_g(s + gslots))
 
     def down_step(b, half, j):
         t = b * 2 * nt + half * nt + j
@@ -168,12 +171,12 @@
         parent = TREES[u][0]
         place = [None if parent[p] is None else _landing(u, parent[p], TREES[u][1][parent[p]].index(p)) for p in range(8)]
         dst, sem = landed(u, c, select(place))
-        target = 2 * select([parent[p] for p in range(8)]) + core
+        target = device(select([parent[p] for p in range(8)]))
         return remote(sbuf.at[c % SBUF, :, columns(u)], dst, upsem.at[c % SBUF, u], sem, target)
 
     def down_copy(u, c, k):
         children = TREES[u][1]
-        target = 2 * select([children[p][k] if k < len(children[p]) else None for p in range(8)]) + core
+        target = device(select([children[p][k] if k < len(children[p]) else None for p in range(8)]))
         piece = fbuf.at[c % FBUF, :, columns(u)]
         return remote(piece, piece, downsem.at[c % FBUF, u, k], bsem.at[c % FBUF, u], target)
 
@@ -248,18 +251,15 @@
         other.wait()
 
     start(load_x(0))
-    start(load_g(0))
-    start(load_g(1))
-    start(load_x(1))
-    for t in range(wslots):
-        start(load_d(t))
+    for s in range(gslots):
+        start(load_g(s))
 
     barrier = pltpu.get_barrier_semaphore()
-    z = pos % 4
+    z = (me // 2) % 4
     rung = (me + 8) % 16
 
-    def greet(device):
-        pl.semaphore_signal(barrier, inc=1, device_id=(dp, device), device_id_type=MESH)
+    def greet(target):
+        pl.semaphore_signal(barrier, inc=1, device_id=(dp, target), device_id_type=MESH)
 
     greet(partner)
     greet(rung)
@@ -279,6 +279,15 @@
     @pl.loop(0, ng)
     def _(g):
         gate_step(0, g)
+
+        @pl.when(g == ng - gslots - 1)
+        def _():
+            for t in range(wslots):
+                start(load_d(t))
+
+        @pl.when(g == ng - gslots)
+        def _():
+            start(load_x(1))
 
     split = (ng + 1) // 2
 
@@ -290,10 +299,6 @@
         @pl.when(b + 2 < nb)
         def _():
             start(load_x(b + 2))
-
-        @pl.when(more)
-        def _():
-            wait(load_x(b + 1))
 
         for half in range(2):
 
@@ -324,6 +329,8 @@
 
                         @pl.when(more)
                         def _(g=g):
+                            if g == 0:
+                                wait(load_x(b + 1))
                             gate_step(b + 1, g)
 
                 elif kind == "S":
@@ -351,8 +358,8 @@
             out_specs=any_spec,
             scratch_shapes=[
                 pltpu.VMEM((2, rows, d), BF16),
-                pltpu.VMEM((2, d, cfg["gw"]), BF16),
-                pltpu.VMEM((2, d, cfg["gw"]), BF16),
+                pltpu.VMEM((3, d, cfg["gw"]), BF16),
+                pltpu.VMEM((3, d, cfg["gw"]), BF16),
                 pltpu.VMEM((4, hidden, cfg["dt"]), BF16),
                 pltpu.VMEM((2, rows, hidden), BF16),
                 pltpu.VMEM((OWN, mine, cfg["half"]), F32),
@@ -363,8 +370,8 @@
                 pltpu.VMEM((RBUF, 6, mine, cfg["yc"]), BF16),
                 pltpu.VMEM((RBUF, 6, mine, cfg["zc"]), BF16),
                 dma((2, 2)),
-                dma((2,)),
-                dma((2,)),
+                dma((3,)),
+                dma((3,)),
                 dma((4,)),
                 dma((STAGE,)),
                 dma((PBUF,)),

time: 313 us -> 307 us (0.981)
  Pallas kernels: 293 us -> 287 us
    pallas_call x1, Pallas kernels: 293 us -> 287 us  [step(): pl.pallas_call(functools.partial(_kernel, cfg), name='mlp', out_shape=jax...]
where the time goes in v3:
time: 307 us
  Pallas kernels  287 us (93%)
  local copies, waits for them, and re-layouts  20.2 us (7%)
    pallas_call x1, Pallas kernels, step(): pl.pallas_call(functools.partial(_kernel, cfg), name='mlp', out_shape=jax...  287 us
    unnamed x1, local copies, waits for them, and re-layouts  20.2 us

profile of v3, /device:TPU:0, one launch (start us, length us, event | category | flops | bytes accessed | tf_op | source)
XLA Modules:
  0.0 306.9 jit_solution(10551710032309680267)
XLA Ops:
  0.0 286.8 %mlp.1 = bf16[2048,7168]{1,0:T(8,128)(2,1)} custom-call(bf16[2048,7168]{1,0:T(8,128)(2,1)} %x_hbm.1, bf16[7168,1280]{1,0:T(8,128)(2,1)} %wg_hbm.1, bf16[7168,1280]{1,0:T(8,128)(2,1)} %wu_hbm.1, bf16[1280,7168]{1,0:T(8,128)(2,1)} %wd_hbm.1), custom_call_target="tpu_custom_call" | custom-call | tf_op jit(solution)/shard_map/mlp/pallas_call | solution.py:353
  286.8 20.2 %copy.6 = bf16[2048,7168]{1,0:T(8,128)(2,1)} copy(bf16[2048,7168]{1,0:T(8,128)(2,1)} %mlp.1) | data formatting | bytes 58720256
